TPU v7x, 32 devices: a whole 2x2x4 slice. The times are simulated.
32 devices in a mesh: patch: 8 (over z, y), sub: 4 (over x, core).
Axes of the slice: x: 2, y: 2, z: 4, core: 2. Of those that a mesh axis runs over, the one named last changes fastest.
Arguments:
- sources: int32 [128, 2], replicated, may hold values from 0 to 16383
- diag_coef: float32 [16384], P(('patch', 'sub')), may hold values from 1 to 2
- tiles: float32 [128, 6, 128, 128], P(('patch', 'sub')), may hold values from -0.109375 to 0.109375
- tile_cols: int32 [128, 6], P(('patch', 'sub')), may hold values from 0 to 7
- send_rows: int32 [32, 4, 128], P(('patch', 'sub')), may hold values from 0 to 511
- recv_rows: int32 [32, 512], P(('patch', 'sub')), may hold values from 0 to 511, each once within a row
- bounds: float32 [2], replicated, may hold values from 0.3 to 3.2, as said below
Outputs:
- solution: float32 [16384, 128], P(('patch', 'sub'))
- res_norm: float32 [128], replicated
Inputs may be any that keep to these rules, and one draw needn't show every extreme that they name: bounds[0] lies in 0.3 to 0.5 and bounds[1] in 2.6 to 3.2.
All inputs are finite; a program needn't handle non-finite values.
Results may differ from a plain program's by a relative error of at most 0.0001.
Values sent between devices are 32-bit elements; how exact they have to be, the bound alone decides.
A program may use at most 64 MiB of HBM per device.

v0:
```python
import jax
import jax.numpy as jnp
from jax import lax
from jax.sharding import PartitionSpec as P

ITERS = 8


def shifted(value, axis, steps):
    count = lax.axis_size(axis)
    pairs = [(source, (source + steps) % count) for source in range(count)]
    return lax.ppermute(value, axis, pairs)


def on_device(sources, diag_coef, tiles, tile_cols, send_rows, recv_rows, bounds):
    rows = diag_coef.shape[0]
    columns = sources.shape[0]
    blk_rows = tiles.shape[0]
    per_row = tiles.shape[1]
    tile_size = tiles.shape[2]
    sends = send_rows[0]
    receives = recv_rows[0]
    device = lax.axis_index("patch") * lax.axis_size("sub") + lax.axis_index("sub")
    local_ids = sources - device * rows
    inside = (local_ids >= 0) & (local_ids < rows)
    which = jnp.arange(columns, dtype=jnp.int32)[:, None]
    flat_index = jnp.where(inside, local_ids * columns + which, rows * columns).reshape(-1)
    counts = jax.ops.segment_sum(
        jnp.ones(flat_index.shape, jnp.float32), flat_index, num_segments=rows * columns + 1
    )
    right_side = counts[: rows * columns].reshape(rows, columns)

    def operate(field):
        packed = field[sends]
        below_patch = shifted(packed[1], "patch", 1)
        above_patch = shifted(packed[0], "patch", -1)
        below_sub = shifted(packed[3], "sub", 1)
        above_sub = shifted(packed[2], "sub", -1)
        received = jnp.concatenate([below_patch, above_patch, below_sub, above_sub], axis=0)
        halo_rows = received[receives]
        extended = jnp.concatenate([field, halo_rows], axis=0).reshape(-1, tile_size, columns)
        summed = jnp.zeros((blk_rows, tile_size, columns), jnp.float32)
        for slot_index in range(per_row):
            summed = summed + jnp.einsum(
                "bij,bjk->bik",
                tiles[:, slot_index],
                extended[tile_cols[:, slot_index]],
                precision=lax.Precision.HIGHEST,
            )
        return diag_coef[:, None] * field + summed.reshape(rows, columns)

    centre = (bounds[0] + bounds[1]) / 2.0
    half_width = (bounds[1] - bounds[0]) / 2.0
    ratio = centre / half_width
    damping = 1.0 / ratio
    solution = jnp.zeros_like(right_side)
    residual = right_side
    direction = right_side / centre
    for iteration in range(ITERS):
        solution = solution + direction
        residual = residual - operate(direction)
        if iteration + 1 < ITERS:
            damping_next = 1.0 / (2.0 * ratio - damping)
            direction = (
                damping_next * damping * direction + 2.0 * damping_next / half_width * residual
            )
            damping = damping_next
    final = right_side - operate(solution)
    squares = lax.psum(jnp.sum(final * final, axis=0), ("patch", "sub"))
    return (solution, jnp.sqrt(squares))


def solution(mesh):
    return jax.shard_map(
        on_device,
        mesh=mesh,
        in_specs=(
            P(),
            P(("patch", "sub")),
            P(("patch", "sub"), None, None, None),
            P(("patch", "sub"), None),
            P(("patch", "sub"), None, None),
            P(("patch", "sub"), None),
            P(),
        ),
        out_specs=(P(("patch", "sub"), None), P()),
        check_vma=False,
    )
```

profile of v0, /device:TPU:0, one launch (start us, length us, event | category | flops | bytes accessed | tf_op | source)
XLA Modules:
  0.0 229.8 jit_solution(4072987159246424181)
XLA Ops:
  4.9 2.3 %scatter_custom_fusion = f32[65537]{0:T(1024)S(1)} fusion(s32[256]{0:T(256)S(1)} %reshape.649, f32[256]{0:T(256)S(1)} %broadcast.65, f32[]{:T(128)} %constant.13.clone.1), kind=kCustom, calls=%fused_computation.254 | custom fusion | flops 256 | bytes 262152 | tf_op jit(solution)/shard_map/scatter-add | solution.py:28
  8.4 3.1 %collective-permute-start = (f32[128,128]{1,0:T(8,128)S(1)}, f32[128,128]{1,0:T(8,128)S(1)}, u32[]{:S(2)}, u32[]{:S(2)}) collective-permute-start(f32[128,128]{1,0:T(8,128)S(1)} %get-tuple-element.42), channel_id=1, source_target_pairs={{0,4},{4,8},{8,12},{12,16},{16,20},{20,24},{24,28},{28,0},{1,5},{5... | collective-permute-start | bytes 196616 | tf_op jit(solution)/shard_map/ppermute | solution.py:12
  11.4 3.1 %collective-permute-start.1 = (f32[128,128]{1,0:T(8,128)S(1)}, f32[128,128]{1,0:T(8,128)S(1)}, u32[]{:S(2)}, u32[]{:S(2)}) collective-permute-start(f32[128,128]{1,0:T(8,128)S(1)} %get-tuple-element.44), channel_id=1, source_target_pairs={{0,28},{4,0},{8,4},{12,8},{16,12},{20,16},{24,20},{28,24},{1,29},{... | collective-permute-start | bytes 196616 | tf_op jit(solution)/shard_map/ppermute | solution.py:12
  14.5 1.7 collective-permute-start.3
  28.8 4.7 %collective-permute-start.5 = (f32[128,128]{1,0:T(8,128)S(1)}, f32[128,128]{1,0:T(8,128)S(1)}, u32[]{:S(2)}, u32[]{:S(2)}) collective-permute-start(f32[128,128]{1,0:T(8,128)S(1)} %get-tuple-element.40), channel_id=1, source_target_pairs={{0,28},{4,0},{8,4},{12,8},{16,12},{20,16},{24,20},{28,24},{1,29},{... | collective-permute-start | bytes 196616 | tf_op jit(solution)/shard_map/ppermute | solution.py:12
  35.7 1.4 collective-permute-done.6
  48.3 1.8 collective-permute-start.10
  50.2 4.7 %collective-permute-start.9 = (f32[128,128]{1,0:T(8,128)S(1)}, f32[128,128]{1,0:T(8,128)S(1)}, u32[]{:S(2)}, u32[]{:S(2)}) collective-permute-start(f32[128,128]{1,0:T(8,128)S(1)} %get-tuple-element.36), channel_id=1, source_target_pairs={{0,28},{4,0},{8,4},{12,8},{16,12},{20,16},{24,20},{28,24},{1,29},{... | collective-permute-start | bytes 196616 | tf_op jit(solution)/shard_map/ppermute | solution.py:12
  55.0 2.3 collective-permute-done.8
  65.8 1.4 convolution_add_fusion.29
  70.0 4.7 %collective-permute-start.13 = (f32[128,128]{1,0:T(8,128)S(1)}, f32[128,128]{1,0:T(8,128)S(1)}, u32[]{:S(2)}, u32[]{:S(2)}) collective-permute-start(f32[128,128]{1,0:T(8,128)S(1)} %get-tuple-element.32), channel_id=1, source_target_pairs={{0,28},{4,0},{8,4},{12,8},{16,12},{20,16},{24,20},{28,24},{1,29},{... | collective-permute-start | bytes 196616 | tf_op jit(solution)/shard_map/ppermute | solution.py:12
  74.8 1.7 collective-permute-start.15
  77.0 1.4 collective-permute-done.14
  78.5 1.6 gather_fusion.25
  88.4 1.4 convolution_add_fusion.24
  93.3 4.7 %collective-permute-start.17 = (f32[128,128]{1,0:T(8,128)}, f32[128,128]{1,0:T(8,128)S(1)}, u32[]{:S(2)}, u32[]{:S(2)}) collective-permute-start(f32[128,128]{1,0:T(8,128)} %get-tuple-element.28), channel_id=1, source_target_pairs={{0,28},{4,0},{8,4},{12,8},{16,12},{20,16},{24,20},{28,24},{1,29},{... | collective-permute-start | bytes 196616 | tf_op jit(solution)/shard_map/ppermute | solution.py:12
  101.8 1.6 gather_fusion.33
  104.4 1.4 gather_fusion.34
  105.8 1.4 gather_fusion.35
  107.2 1.4 gather_fusion.36
  108.5 1.4 gather_fusion.37
  109.9 1.4 gather_fusion.38
  111.3 1.4 gather_fusion.39
  112.7 1.4 fusion.46
  114.1 1.4 convolution_add_fusion.19
  119.7 4.7 %collective-permute-start.21 = (f32[128,128]{1,0:T(8,128)S(1)}, f32[128,128]{1,0:T(8,128)S(1)}, u32[]{:S(2)}, u32[]{:S(2)}) collective-permute-start(f32[128,128]{1,0:T(8,128)S(1)} %get-tuple-element.24), channel_id=1, source_target_pairs={{0,28},{4,0},{8,4},{12,8},{16,12},{20,16},{24,20},{28,24},{1,29},{... | collective-permute-start | bytes 196616 | tf_op jit(solution)/shard_map/ppermute | solution.py:12
  129.0 1.6 gather_fusion.41
  132.3 1.4 gather_fusion.43
  133.7 1.4 gather_fusion.44
  135.1 1.4 gather_fusion.45
  136.4 1.4 gather_fusion.46
  137.8 1.4 gather_fusion.47
  139.6 1.4 convolution_add_fusion.14
  145.2 4.7 %collective-permute-start.25 = (f32[128,128]{1,0:T(8,128)S(1)}, f32[128,128]{1,0:T(8,128)S(1)}, u32[]{:S(2)}, u32[]{:S(2)}) collective-permute-start(f32[128,128]{1,0:T(8,128)S(1)} %get-tuple-element.20), channel_id=1, source_target_pairs={{0,28},{4,0},{8,4},{12,8},{16,12},{20,16},{24,20},{28,24},{1,29},{... | collective-permute-start | bytes 196616 | tf_op jit(solution)/shard_map/ppermute | solution.py:12
  154.5 1.6 gather_fusion.49
  157.8 1.4 gather_fusion.51
  159.2 1.4 gather_fusion.52
  160.6 1.4 gather_fusion.53
  162.0 1.4 gather_fusion.54
  163.3 1.4 gather_fusion.55
  165.1 1.4 convolution_add_fusion.9
  169.6 4.7 %collective-permute-start.29 = (f32[128,128]{1,0:T(8,128)S(1)}, f32[128,128]{1,0:T(8,128)S(1)}, u32[]{:S(2)}, u32[]{:S(2)}) collective-permute-start(f32[128,128]{1,0:T(8,128)S(1)} %get-tuple-element.16), channel_id=1, source_target_pairs={{0,28},{4,0},{8,4},{12,8},{16,12},{20,16},{24,20},{28,24},{1,29},{... | collective-permute-start | bytes 196616 | tf_op jit(solution)/shard_map/ppermute | solution.py:12
  176.5 1.4 collective-permute-done.30
  179.8 1.4 gather_fusion.59
  181.2 1.4 gather_fusion.60
  182.6 1.4 gather_fusion.61
  184.0 1.4 gather_fusion.62
  190.5 38.8 %psum.7 = f32[128]{0:T(128)S(1)} all-reduce(f32[128]{0:T(128)S(1)} %fusion.58), channel_id=1, replica_groups=mesh['patch'=8,'sub'=4] {'patch','sub'}, use_global_device_ids=true, to_apply=%region_2.3 | all-reduce | flops 128 | bytes 1024 | tf_op jit(solution)/shard_map/psum | solution.py:69
  (265 shorter events, 89.6 us)
Async XLA Ops:
  7.2 20.3 %copy-start.2 = (f32[65537]{0:T(1024)}, f32[65537]{0:T(1024)S(1)}, u32[]{:S(2)}) copy-start(f32[65537]{0:T(1024)S(1)} %scatter_custom_fusion) | copy-start | bytes 786448
  7.3 10.4 %copy-start.43 = (s32[1,512]{1,0:T(1,128)S(1)}, s32[1,512]{1,0:T(1,128)}, u32[]{:S(2)}) copy-start(s32[1,512]{1,0:T(1,128)} %param.12) | copy-start | bytes 6148
  7.3 10.4 %copy-start.36 = (s32[4,6]{1,0:T(4,128)S(1)}, s32[4,6]{1,0:T(4,128)}, u32[]{:S(2)}) copy-start(s32[4,6]{1,0:T(4,128)} %param.10) | copy-start | bytes 292
  8.4 9.8 %collective-permute-start = (f32[128,128]{1,0:T(8,128)S(1)}, f32[128,128]{1,0:T(8,128)S(1)}, u32[]{:S(2)}, u32[]{:S(2)}) collective-permute-start(f32[128,128]{1,0:T(8,128)S(1)} %get-tuple-element.42), channel_id=1, source_target_pairs={{0,4},{4,8},{8,12},{12,16},{16,20},{20,24},{24,28},{28,0},{1,5},{5... | collective-permute-start | bytes 196616 | tf_op jit(solution)/shard_map/ppermute | solution.py:12
  11.4 6.7 %collective-permute-start.1 = (f32[128,128]{1,0:T(8,128)S(1)}, f32[128,128]{1,0:T(8,128)S(1)}, u32[]{:S(2)}, u32[]{:S(2)}) collective-permute-start(f32[128,128]{1,0:T(8,128)S(1)} %get-tuple-element.44), channel_id=1, source_target_pairs={{0,28},{4,0},{8,4},{12,8},{16,12},{20,16},{24,20},{28,24},{1,29},{... | collective-permute-start | bytes 196616 | tf_op jit(solution)/shard_map/ppermute | solution.py:12
  14.5 3.7 %collective-permute-start.2 = (f32[128,128]{1,0:T(8,128)S(1)}, f32[128,128]{1,0:T(8,128)S(1)}, u32[]{:S(2)}, u32[]{:S(2)}) collective-permute-start(f32[128,128]{1,0:T(8,128)S(1)} %get-tuple-element.43), channel_id=1, source_target_pairs={{0,1},{1,2},{2,3},{3,0},{4,5},{5,6},{6,7},{7,4},{8,9},{9,10},{10,1... | collective-permute-start | bytes 196616 | tf_op jit(solution)/shard_map/ppermute | solution.py:12
  14.5 3.7 %collective-permute-start.3 = (f32[128,128]{1,0:T(8,128)S(1)}, f32[128,128]{1,0:T(8,128)S(1)}, u32[]{:S(2)}, u32[]{:S(2)}) collective-permute-start(f32[128,128]{1,0:T(8,128)S(1)} %get-tuple-element.45), channel_id=1, source_target_pairs={{0,3},{1,0},{2,1},{3,2},{4,7},{5,4},{6,5},{7,6},{8,11},{9,8},{10,9... | collective-permute-start | bytes 196616 | tf_op jit(solution)/shard_map/ppermute | solution.py:12
  18.0 63.1 %copy-start.38 = (s32[1024]{0:T(1024)}, s32[1024]{0:T(1024)S(1)}, u32[]{:S(2)}) copy-start(s32[1024]{0:T(1024)S(1)} %get-tuple-element.53) | copy-start | bytes 12292
  18.1 63.6 %copy-start.37 = (s32[1024]{0:T(1024)}, s32[1024]{0:T(1024)S(1)}, u32[]{:S(2)}) copy-start(s32[1024]{0:T(1024)S(1)} %get-tuple-element.52) | copy-start | bytes 12292
  18.1 64.9 %copy-start.40 = (s32[1024]{0:T(1024)}, s32[1024]{0:T(1024)S(1)}, u32[]{:S(2)}) copy-start(s32[1024]{0:T(1024)S(1)} %get-tuple-element.51) | copy-start | bytes 12292
  18.1 66.2 %copy-start.39 = (s32[1024]{0:T(1024)}, s32[1024]{0:T(1024)S(1)}, u32[]{:S(2)}) copy-start(s32[1024]{0:T(1024)S(1)} %get-tuple-element.50) | copy-start | bytes 12292
  18.1 67.4 %copy-start.42 = (s32[1024]{0:T(1024)}, s32[1024]{0:T(1024)S(1)}, u32[]{:S(2)}) copy-start(s32[1024]{0:T(1024)S(1)} %get-tuple-element.49) | copy-start | bytes 12292
  18.1 68.6 %copy-start.41 = (s32[1024]{0:T(1024)}, s32[1024]{0:T(1024)S(1)}, u32[]{:S(2)}) copy-start(s32[1024]{0:T(1024)S(1)} %get-tuple-element.48) | copy-start | bytes 12292
  19.3 4.8 %copy-start = (f32[4,6,128,128]{3,2,1,0:T(8,128)S(1)}, f32[4,6,128,128]{3,2,1,0:T(8,128)}, u32[]{:S(2)}) copy-start(f32[4,6,128,128]{3,2,1,0:T(8,128)} %param.9) | copy-start | bytes 4718596
  28.7 7.0 %collective-permute-start.4 = (f32[128,128]{1,0:T(8,128)S(1)}, f32[128,128]{1,0:T(8,128)S(1)}, u32[]{:S(2)}, u32[]{:S(2)}) collective-permute-start(f32[128,128]{1,0:T(8,128)S(1)} %get-tuple-element.38), channel_id=1, source_target_pairs={{0,4},{4,8},{8,12},{12,16},{16,20},{20,24},{24,28},{28,0},{1,5},{5... | collective-permute-start | bytes 196616 | tf_op jit(solution)/shard_map/ppermute | solution.py:12
  28.8 7.0 %collective-permute-start.5 = (f32[128,128]{1,0:T(8,128)S(1)}, f32[128,128]{1,0:T(8,128)S(1)}, u32[]{:S(2)}, u32[]{:S(2)}) collective-permute-start(f32[128,128]{1,0:T(8,128)S(1)} %get-tuple-element.40), channel_id=1, source_target_pairs={{0,28},{4,0},{8,4},{12,8},{16,12},{20,16},{24,20},{28,24},{1,29},{... | collective-permute-start | bytes 196616 | tf_op jit(solution)/shard_map/ppermute | solution.py:12
  33.5 3.7 %collective-permute-start.6 = (f32[128,128]{1,0:T(8,128)S(1)}, f32[128,128]{1,0:T(8,128)S(1)}, u32[]{:S(2)}, u32[]{:S(2)}) collective-permute-start(f32[128,128]{1,0:T(8,128)S(1)} %get-tuple-element.39), channel_id=1, source_target_pairs={{0,1},{1,2},{2,3},{3,0},{4,5},{5,6},{6,7},{7,4},{8,9},{9,10},{10,1... | collective-permute-start | bytes 196616 | tf_op jit(solution)/shard_map/ppermute | solution.py:12
  34.7 2.5 %collective-permute-start.7 = (f32[128,128]{1,0:T(8,128)S(1)}, f32[128,128]{1,0:T(8,128)S(1)}, u32[]{:S(2)}, u32[]{:S(2)}) collective-permute-start(f32[128,128]{1,0:T(8,128)S(1)} %get-tuple-element.41), channel_id=1, source_target_pairs={{0,3},{1,0},{2,1},{3,2},{4,7},{5,4},{6,5},{7,6},{8,11},{9,8},{10,9... | collective-permute-start | bytes 196616 | tf_op jit(solution)/shard_map/ppermute | solution.py:12
  48.3 6.7 %collective-permute-start.10 = (f32[128,128]{1,0:T(8,128)S(1)}, f32[128,128]{1,0:T(8,128)S(1)}, u32[]{:S(2)}, u32[]{:S(2)}) collective-permute-start(f32[128,128]{1,0:T(8,128)S(1)} %get-tuple-element.35), channel_id=1, source_target_pairs={{0,1},{1,2},{2,3},{3,0},{4,5},{5,6},{6,7},{7,4},{8,9},{9,10},{10,1... | collective-permute-start | bytes 196616 | tf_op jit(solution)/shard_map/ppermute | solution.py:12
  50.1 4.9 %collective-permute-start.11 = (f32[128,128]{1,0:T(8,128)S(1)}, f32[128,128]{1,0:T(8,128)S(1)}, u32[]{:S(2)}, u32[]{:S(2)}) collective-permute-start(f32[128,128]{1,0:T(8,128)S(1)} %get-tuple-element.37), channel_id=1, source_target_pairs={{0,3},{1,0},{2,1},{3,2},{4,7},{5,4},{6,5},{7,6},{8,11},{9,8},{10,9... | collective-permute-start | bytes 196616 | tf_op jit(solution)/shard_map/ppermute | solution.py:12
  50.2 7.1 %collective-permute-start.8 = (f32[128,128]{1,0:T(8,128)S(1)}, f32[128,128]{1,0:T(8,128)S(1)}, u32[]{:S(2)}, u32[]{:S(2)}) collective-permute-start(f32[128,128]{1,0:T(8,128)S(1)} %get-tuple-element.34), channel_id=1, source_target_pairs={{0,4},{4,8},{8,12},{12,16},{16,20},{20,24},{24,28},{28,0},{1,5},{5... | collective-permute-start | bytes 196616 | tf_op jit(solution)/shard_map/ppermute | solution.py:12
  50.2 7.1 %collective-permute-start.9 = (f32[128,128]{1,0:T(8,128)S(1)}, f32[128,128]{1,0:T(8,128)S(1)}, u32[]{:S(2)}, u32[]{:S(2)}) collective-permute-start(f32[128,128]{1,0:T(8,128)S(1)} %get-tuple-element.36), channel_id=1, source_target_pairs={{0,28},{4,0},{8,4},{12,8},{16,12},{20,16},{24,20},{28,24},{1,29},{... | collective-permute-start | bytes 196616 | tf_op jit(solution)/shard_map/ppermute | solution.py:12
  70.0 7.0 %collective-permute-start.12 = (f32[128,128]{1,0:T(8,128)S(1)}, f32[128,128]{1,0:T(8,128)S(1)}, u32[]{:S(2)}, u32[]{:S(2)}) collective-permute-start(f32[128,128]{1,0:T(8,128)S(1)} %get-tuple-element.30), channel_id=1, source_target_pairs={{0,4},{4,8},{8,12},{12,16},{16,20},{20,24},{24,28},{28,0},{1,5},{5... | collective-permute-start | bytes 196616 | tf_op jit(solution)/shard_map/ppermute | solution.py:12
  70.0 7.0 %collective-permute-start.13 = (f32[128,128]{1,0:T(8,128)S(1)}, f32[128,128]{1,0:T(8,128)S(1)}, u32[]{:S(2)}, u32[]{:S(2)}) collective-permute-start(f32[128,128]{1,0:T(8,128)S(1)} %get-tuple-element.32), channel_id=1, source_target_pairs={{0,28},{4,0},{8,4},{12,8},{16,12},{20,16},{24,20},{28,24},{1,29},{... | collective-permute-start | bytes 196616 | tf_op jit(solution)/shard_map/ppermute | solution.py:12
  74.8 3.7 %collective-permute-start.14 = (f32[128,128]{1,0:T(8,128)S(1)}, f32[128,128]{1,0:T(8,128)S(1)}, u32[]{:S(2)}, u32[]{:S(2)}) collective-permute-start(f32[128,128]{1,0:T(8,128)S(1)} %get-tuple-element.31), channel_id=1, source_target_pairs={{0,1},{1,2},{2,3},{3,0},{4,5},{5,6},{6,7},{7,4},{8,9},{9,10},{10,1... | collective-permute-start | bytes 196616 | tf_op jit(solution)/shard_map/ppermute | solution.py:12
  74.8 3.7 %collective-permute-start.15 = (f32[128,128]{1,0:T(8,128)S(1)}, f32[128,128]{1,0:T(8,128)S(1)}, u32[]{:S(2)}, u32[]{:S(2)}) collective-permute-start(f32[128,128]{1,0:T(8,128)S(1)} %get-tuple-element.33), channel_id=1, source_target_pairs={{0,3},{1,0},{2,1},{3,2},{4,7},{5,4},{6,5},{7,6},{8,11},{9,8},{10,9... | collective-permute-start | bytes 196616 | tf_op jit(solution)/shard_map/ppermute | solution.py:12
  93.3 7.2 %collective-permute-start.16 = (f32[128,128]{1,0:T(8,128)}, f32[128,128]{1,0:T(8,128)S(1)}, u32[]{:S(2)}, u32[]{:S(2)}) collective-permute-start(f32[128,128]{1,0:T(8,128)} %get-tuple-element.26), channel_id=1, source_target_pairs={{0,4},{4,8},{8,12},{12,16},{16,20},{20,24},{24,28},{28,0},{1,5},{5... | collective-permute-start | bytes 196616 | tf_op jit(solution)/shard_map/ppermute | solution.py:12
  93.3 7.2 %collective-permute-start.17 = (f32[128,128]{1,0:T(8,128)}, f32[128,128]{1,0:T(8,128)S(1)}, u32[]{:S(2)}, u32[]{:S(2)}) collective-permute-start(f32[128,128]{1,0:T(8,128)} %get-tuple-element.28), channel_id=1, source_target_pairs={{0,28},{4,0},{8,4},{12,8},{16,12},{20,16},{24,20},{28,24},{1,29},{... | collective-permute-start | bytes 196616 | tf_op jit(solution)/shard_map/ppermute | solution.py:12
  98.0 3.7 %collective-permute-start.18 = (f32[128,128]{1,0:T(8,128)S(1)}, f32[128,128]{1,0:T(8,128)S(1)}, u32[]{:S(2)}, u32[]{:S(2)}) collective-permute-start(f32[128,128]{1,0:T(8,128)S(1)} %get-tuple-element.27), channel_id=1, source_target_pairs={{0,1},{1,2},{2,3},{3,0},{4,5},{5,6},{6,7},{7,4},{8,9},{9,10},{10,1... | collective-permute-start | bytes 196616 | tf_op jit(solution)/shard_map/ppermute | solution.py:12
  99.1 2.6 %collective-permute-start.19 = (f32[128,128]{1,0:T(8,128)S(1)}, f32[128,128]{1,0:T(8,128)S(1)}, u32[]{:S(2)}, u32[]{:S(2)}) collective-permute-start(f32[128,128]{1,0:T(8,128)S(1)} %get-tuple-element.29), channel_id=1, source_target_pairs={{0,3},{1,0},{2,1},{3,2},{4,7},{5,4},{6,5},{7,6},{8,11},{9,8},{10,9... | collective-permute-start | bytes 196616 | tf_op jit(solution)/shard_map/ppermute | solution.py:12
  112.7 2.8 %copy-start.32 = (f32[4,128,128]{2,1,0:T(8,128)S(1)}, f32[4,128,128]{2,1,0:T(8,128)}, u32[]{:S(2)}) copy-start(f32[4,128,128]{2,1,0:T(8,128)} %gather_fusion.36) | copy-start | bytes 786436
  112.7 3.2 %copy-start.26 = (f32[4,128,128]{2,1,0:T(8,128)S(1)}, f32[4,128,128]{2,1,0:T(8,128)}, u32[]{:S(2)}) copy-start(f32[4,128,128]{2,1,0:T(8,128)} %gather_fusion.37) | copy-start | bytes 786436
  119.7 7.2 %collective-permute-start.20 = (f32[128,128]{1,0:T(8,128)}, f32[128,128]{1,0:T(8,128)S(1)}, u32[]{:S(2)}, u32[]{:S(2)}) collective-permute-start(f32[128,128]{1,0:T(8,128)} %get-tuple-element.22), channel_id=1, source_target_pairs={{0,4},{4,8},{8,12},{12,16},{16,20},{20,24},{24,28},{28,0},{1,5},{5... | collective-permute-start | bytes 196616 | tf_op jit(solution)/shard_map/ppermute | solution.py:12
  119.7 7.2 %collective-permute-start.21 = (f32[128,128]{1,0:T(8,128)S(1)}, f32[128,128]{1,0:T(8,128)S(1)}, u32[]{:S(2)}, u32[]{:S(2)}) collective-permute-start(f32[128,128]{1,0:T(8,128)S(1)} %get-tuple-element.24), channel_id=1, source_target_pairs={{0,28},{4,0},{8,4},{12,8},{16,12},{20,16},{24,20},{28,24},{1,29},{... | collective-permute-start | bytes 196616 | tf_op jit(solution)/shard_map/ppermute | solution.py:12
  124.4 3.7 %collective-permute-start.22 = (f32[128,128]{1,0:T(8,128)S(1)}, f32[128,128]{1,0:T(8,128)S(1)}, u32[]{:S(2)}, u32[]{:S(2)}) collective-permute-start(f32[128,128]{1,0:T(8,128)S(1)} %get-tuple-element.23), channel_id=1, source_target_pairs={{0,1},{1,2},{2,3},{3,0},{4,5},{5,6},{6,7},{7,4},{8,9},{9,10},{10,1... | collective-permute-start | bytes 196616 | tf_op jit(solution)/shard_map/ppermute | solution.py:12
  125.5 2.6 %collective-permute-start.23 = (f32[128,128]{1,0:T(8,128)S(1)}, f32[128,128]{1,0:T(8,128)}, u32[]{:S(2)}, u32[]{:S(2)}) collective-permute-start(f32[128,128]{1,0:T(8,128)S(1)} %get-tuple-element.25), channel_id=1, source_target_pairs={{0,3},{1,0},{2,1},{3,2},{4,7},{5,4},{6,5},{7,6},{8,11},{9,8},{10,9... | collective-permute-start | bytes 196616 | tf_op jit(solution)/shard_map/ppermute | solution.py:12
  145.2 7.2 %collective-permute-start.24 = (f32[128,128]{1,0:T(8,128)}, f32[128,128]{1,0:T(8,128)S(1)}, u32[]{:S(2)}, u32[]{:S(2)}) collective-permute-start(f32[128,128]{1,0:T(8,128)} %get-tuple-element.18), channel_id=1, source_target_pairs={{0,4},{4,8},{8,12},{12,16},{16,20},{20,24},{24,28},{28,0},{1,5},{5... | collective-permute-start | bytes 196616 | tf_op jit(solution)/shard_map/ppermute | solution.py:12
  145.2 7.2 %collective-permute-start.25 = (f32[128,128]{1,0:T(8,128)S(1)}, f32[128,128]{1,0:T(8,128)S(1)}, u32[]{:S(2)}, u32[]{:S(2)}) collective-permute-start(f32[128,128]{1,0:T(8,128)S(1)} %get-tuple-element.20), channel_id=1, source_target_pairs={{0,28},{4,0},{8,4},{12,8},{16,12},{20,16},{24,20},{28,24},{1,29},{... | collective-permute-start | bytes 196616 | tf_op jit(solution)/shard_map/ppermute | solution.py:12
  149.9 3.7 %collective-permute-start.26 = (f32[128,128]{1,0:T(8,128)S(1)}, f32[128,128]{1,0:T(8,128)S(1)}, u32[]{:S(2)}, u32[]{:S(2)}) collective-permute-start(f32[128,128]{1,0:T(8,128)S(1)} %get-tuple-element.19), channel_id=1, source_target_pairs={{0,1},{1,2},{2,3},{3,0},{4,5},{5,6},{6,7},{7,4},{8,9},{9,10},{10,1... | collective-permute-start | bytes 196616 | tf_op jit(solution)/shard_map/ppermute | solution.py:12
  151.1 2.5 %collective-permute-start.27 = (f32[128,128]{1,0:T(8,128)S(1)}, f32[128,128]{1,0:T(8,128)}, u32[]{:S(2)}, u32[]{:S(2)}) collective-permute-start(f32[128,128]{1,0:T(8,128)S(1)} %get-tuple-element.21), channel_id=1, source_target_pairs={{0,3},{1,0},{2,1},{3,2},{4,7},{5,4},{6,5},{7,6},{8,11},{9,8},{10,9... | collective-permute-start | bytes 196616 | tf_op jit(solution)/shard_map/ppermute | solution.py:12
  165.1 2.2 copy-start.21
  168.4 21.9 %copy-start.1 = (f32[512,128]{1,0:T(8,128)}, f32[512,128]{1,0:T(8,128)S(1)}, u32[]{:S(2)}) copy-start(f32[512,128]{1,0:T(8,128)S(1)} %fusion.62) | copy-start | bytes 786436
  169.5 7.0 %collective-permute-start.28 = (f32[128,128]{1,0:T(8,128)S(1)}, f32[128,128]{1,0:T(8,128)S(1)}, u32[]{:S(2)}, u32[]{:S(2)}) collective-permute-start(f32[128,128]{1,0:T(8,128)S(1)} %get-tuple-element.14), channel_id=1, source_target_pairs={{0,4},{4,8},{8,12},{12,16},{16,20},{20,24},{24,28},{28,0},{1,5},{5... | collective-permute-start | bytes 196616 | tf_op jit(solution)/shard_map/ppermute | solution.py:12
  169.6 7.0 %collective-permute-start.29 = (f32[128,128]{1,0:T(8,128)S(1)}, f32[128,128]{1,0:T(8,128)S(1)}, u32[]{:S(2)}, u32[]{:S(2)}) collective-permute-start(f32[128,128]{1,0:T(8,128)S(1)} %get-tuple-element.16), channel_id=1, source_target_pairs={{0,28},{4,0},{8,4},{12,8},{16,12},{20,16},{24,20},{28,24},{1,29},{... | collective-permute-start | bytes 196616 | tf_op jit(solution)/shard_map/ppermute | solution.py:12
  174.3 3.7 %collective-permute-start.30 = (f32[128,128]{1,0:T(8,128)S(1)}, f32[128,128]{1,0:T(8,128)S(1)}, u32[]{:S(2)}, u32[]{:S(2)}) collective-permute-start(f32[128,128]{1,0:T(8,128)S(1)} %get-tuple-element.15), channel_id=1, source_target_pairs={{0,1},{1,2},{2,3},{3,0},{4,5},{5,6},{6,7},{7,4},{8,9},{9,10},{10,1... | collective-permute-start | bytes 196616 | tf_op jit(solution)/shard_map/ppermute | solution.py:12
  175.5 2.5 %collective-permute-start.31 = (f32[128,128]{1,0:T(8,128)S(1)}, f32[128,128]{1,0:T(8,128)S(1)}, u32[]{:S(2)}, u32[]{:S(2)}) collective-permute-start(f32[128,128]{1,0:T(8,128)S(1)} %get-tuple-element.17), channel_id=1, source_target_pairs={{0,3},{1,0},{2,1},{3,2},{4,7},{5,4},{6,5},{7,6},{8,11},{9,8},{10,9... | collective-permute-start | bytes 196616 | tf_op jit(solution)/shard_map/ppermute | solution.py:12
  186.1 3.1 %copy-start.16 = (f32[4,128,128]{2,1,0:T(8,128)S(1)}, f32[4,128,128]{2,1,0:T(8,128)}, u32[]{:S(2)}) copy-start(f32[4,128,128]{2,1,0:T(8,128)} %gather_fusion.61) | copy-start | bytes 786436
  186.4 3.1 %copy-start.15 = (f32[4,128,128]{2,1,0:T(8,128)S(1)}, f32[4,128,128]{2,1,0:T(8,128)}, u32[]{:S(2)}) copy-start(f32[4,128,128]{2,1,0:T(8,128)} %gather_fusion.62) | copy-start | bytes 786436
  (28 other events, 46.2 us)
where the time goes:
time: 231 us; the launch traced here: 230 us
  local copies, waits for them, and re-layouts  78.7 us (34%)
  starting transfers between devices  53.4 us (23%)
  blocking collectives  38.8 us (17%)
  matrix products  28 us (12%)
  waiting for transfers between devices  13.6 us (6%)
  other arithmetic  11.9 us (5%)
  between operations  5.44 us (2%)
    gather x48, local copies, waits for them, and re-layouts, operate(): extended[tile_cols[:, slot_index]]  54.6 us
    ppermute x32, starting transfers between devices, shifted(): return lax.ppermute(value, axis, pairs)  53.4 us
    psum x1, blocking collectives, on_device(): squares = lax.psum(jnp.sum(final * final, axis=0), ('patch', 'sub'))  38.8 us
    dot_general x48, matrix products, operate(): jnp.einsum('bij,bjk->bik', tiles[:, slot_index], extended[tile_cols[:, sl...  28 us
    ppermute x32, waiting for transfers between devices, shifted(): return lax.ppermute(value, axis, pairs)  13.6 us
    gather x8, local copies, waits for them, and re-layouts, operate(): halo_rows = received[receives]  10.7 us
    gather x8, local copies, waits for them, and re-layouts, operate(): packed = field[sends]  8.28 us
  transfers between devices with their start and end apart: 32, of which 13 were waited for; matrix products, arithmetic and copies ran while one was open for 0% of the time, Pallas kernels for 0%

commit v1 on v0

v1 whole, which is shorter than its diff:
```python
import functools

import jax
import jax.numpy as jnp
from jax import lax
from jax.experimental import pallas as pl
from jax.experimental.pallas import tpu as pltpu
from jax.sharding import PartitionSpec as P

ITERS = 8
MESH = pl.DeviceIdType.MESH
F32 = jnp.float32
BF16 = jnp.bfloat16


def halves(value):
    high = value.astype(BF16)
    return high, (value - high.astype(F32)).astype(BF16)


def product(high, low, pair, columns):
    wide = jnp.dot(high, pair, preferred_element_type=F32)
    narrow = jnp.dot(low, pair[:, :columns], preferred_element_type=F32)
    return wide[:, :columns] + wide[:, columns:] + narrow


def kernel(
    n_patch, n_sub,
    sources_ref, diag_ref, tiles_hbm, cols_ref, sends_ref, receives_ref, bounds_ref,
    solution_ref, norm_ref,
    tiles_ref, near_hi, near_lo, far_hi, far_lo, halo_hi, halo_lo,
    direction_ref, residual_ref, packed_residual, total_ref, pair_ref, heard_pair,
    packed_ref, heard_ref, heard_rows, norms_ref,
    tile_sems, row_send, row_recv, send_sems, recv_sems, norm_send, norm_recv,
):
    blk_rows, per_row, size, _ = tiles_hbm.shape
    rows = blk_rows * size
    n_src, columns = sources_ref.shape
    sent = sends_ref.shape[2]
    halo = receives_ref.shape[1]
    packed_rows = 4 * sent
    patch, sub = lax.axis_index("patch"), lax.axis_index("sub")
    devices = n_patch * n_sub
    me = patch * n_sub + sub

    copies = [
        pltpu.make_async_copy(tiles_hbm.at[b], tiles_ref.at[b], tile_sems.at[b])
        for b in range(blk_rows)
    ]
    for copy in copies:
        copy.start()

    barrier = pltpu.get_barrier_semaphore()

    @pl.loop(1, devices)
    def _(step):
        other = lax.rem(me + step, devices)
        pl.semaphore_signal(
            barrier, inc=1, device_id=(other // n_sub, lax.rem(other, n_sub)), device_id_type=MESH
        )

    lower_patch = lax.rem(patch + n_patch - 1, n_patch)
    upper_patch = lax.rem(patch + 1, n_patch)
    lower_sub = lax.rem(sub + n_sub - 1, n_sub)
    upper_sub = lax.rem(sub + 1, n_sub)
    targets = [(lower_patch, sub), (upper_patch, sub), (patch, lower_sub), (patch, upper_sub)]
    lands = [1, 0, 3, 2]
    origins = [targets[0], targets[1], targets[2], targets[3]]

    low_end = jnp.full((1, columns), bounds_ref[0], F32)
    high_end = jnp.full((1, columns), bounds_ref[1], F32)
    centre = (low_end + high_end) / 2.0
    half_width = (high_end - low_end) / 2.0
    ratio = centre / half_width

    def counted(ids):
        total = jnp.zeros(ids.shape, F32)
        for s in range(n_src):
            total = total + jnp.where(sources_ref[s : s + 1, :] == ids, 1.0, 0.0)
        return total

    right_side = counted(me * rows + lax.broadcasted_iota(jnp.int32, (rows, columns), 0))
    direction = right_side / centre
    residual_ref[...] = right_side
    direction_ref[...] = direction
    solution_ref[...] = direction
    high, low = halves(direction)
    pair_ref[:, :columns] = high
    pair_ref[:, columns:] = low

    def as_column(row, width):
        return jnp.broadcast_to(row, (width, row.shape[1])).T

    picks = []
    for j in range(4):
        column = as_column(sends_ref[j], columns)
        mine = counted(me * rows + column)
        packed_residual[pl.ds(j * sent, sent)] = mine
        packed_ref[0, j] = mine / centre
        wide = as_column(sends_ref[j], rows)
        picks.append(
            jnp.where(wide == lax.broadcasted_iota(jnp.int32, (sent, rows), 1), 1.0, 0.0).astype(BF16)
        )
    pick = jnp.concatenate(picks, axis=0)
    place = jnp.where(
        receives_ref[...] == lax.broadcasted_iota(jnp.int32, (packed_rows, halo), 0), 1.0, 0.0
    ).astype(BF16)

    pl.semaphore_wait(barrier, devices - 1)
    row_copies = []
    for j in range(4):
        copy = pltpu.make_async_remote_copy(
            src_ref=sends_ref.at[j], dst_ref=heard_rows.at[lands[j]],
            send_sem=row_send.at[j], recv_sem=row_recv.at[lands[j]],
            device_id=targets[j], device_id_type=MESH,
        )
        copy.start()
        row_copies.append(copy)

    eye = lax.broadcasted_iota(jnp.int32, (size, size), 0) == lax.broadcasted_iota(
        jnp.int32, (size, size), 1
    )
    for b in range(blk_rows):
        copies[b].wait()
        for c in range(blk_rows + halo // size):
            block = jnp.zeros((size, size), F32)
            for n in range(per_row):
                block = block + tiles_ref[b, n] * (cols_ref[b, n] == c).astype(F32)
            if c == b:
                block = block + jnp.where(eye, diag_ref[b : b + 1, :], 0.0)
            high, low = halves(block)
            at = pl.ds(packed_rows + b * size, size)
            if c < blk_rows:
                near_hi[at, pl.ds(c * size, size)] = high
                near_lo[at, pl.ds(c * size, size)] = low
            else:
                place_at = pl.ds((c - blk_rows) * size, size)
                halo_hi[pl.ds(b * size, size), place_at] = high
                halo_lo[pl.ds(b * size, size), place_at] = low
    own = pl.ds(packed_rows, rows)
    first = pl.ds(0, packed_rows)
    for halo_part, far, near in ((halo_hi, far_hi, near_hi), (halo_lo, far_lo, near_lo)):
        far[own] = lax.dot_general(
            halo_part[...], place, (((1,), (1,)), ((), ())), preferred_element_type=F32
        ).astype(BF16)
        far[first] = jnp.dot(pick, far[own], preferred_element_type=F32).astype(BF16)
        near[first] = jnp.dot(pick, near[own], preferred_element_type=F32).astype(BF16)

    for j in range(4):
        row_copies[j].wait()
    for j in range(4):
        base = (origins[j][0] * n_sub + origins[j][1]) * rows
        value = counted(base + as_column(heard_rows[j], columns)) / centre
        high, low = halves(value)
        heard_pair[pl.ds(j * sent, sent), :columns] = high
        heard_pair[pl.ds(j * sent, sent), columns:] = low

    def exchange(slot, j):
        return pltpu.make_async_remote_copy(
            src_ref=packed_ref.at[slot, j], dst_ref=heard_ref.at[slot, lands[j]],
            send_sem=send_sems.at[slot, j], recv_sem=recv_sems.at[slot, lands[j]],
            device_id=targets[j], device_id_type=MESH,
        )

    def arrival(slot, j):
        return pltpu.make_async_remote_copy(
            src_ref=packed_ref.at[slot, j], dst_ref=heard_ref.at[slot, j],
            send_sem=send_sems.at[slot, j], recv_sem=recv_sems.at[slot, j],
            device_id=targets[j], device_id_type=MESH,
        )

    patch_part, sub_part = pl.ds(0, 2 * sent), pl.ds(2 * sent, 2 * sent)

    def listen(slot, pieces):
        for j in pieces:
            arrival(slot, j).wait_recv()
            high, low = halves(heard_ref[slot, j])
            heard_pair[pl.ds(j * sent, sent), :columns] = high
            heard_pair[pl.ds(j * sent, sent), columns:] = low

    def far_product(at, part):
        return product(far_hi[at, part], far_lo[at, part], heard_pair[part], columns)

    def step(slot, damping, last, heard):
        at = own if last else pl.ds(0, packed_rows + rows)
        total_ref[at] = product(near_hi[at], near_lo[at], pair_ref[...], columns)
        if heard:
            listen(slot, (2, 3))
        total_ref[at] = total_ref[at] + far_product(at, sub_part)
        if heard:
            listen(slot, (0, 1))
        if last:
            residual_ref[...] = residual_ref[...] - (total_ref[own] + far_product(own, patch_part))
            return damping
        damping_next = 1.0 / (2.0 * ratio - damping)
        keep = damping_next * damping
        gain = 2.0 * damping_next / half_width
        for group in (0, 2):
            span = pl.ds(group * sent, 2 * sent)
            update = total_ref[span] + far_product(span, patch_part)
            rest = packed_residual[span] - update
            packed_residual[span] = rest
            for i in range(2):
                j = group + i
                packed_ref[slot + 1, j] = (
                    keep * packed_ref[slot, j] + gain * rest[i * sent : (i + 1) * sent]
                )
                exchange(slot + 1, j).start()
        residual = residual_ref[...] - (total_ref[own] + far_product(own, patch_part))
        residual_ref[...] = residual
        direction = keep * direction_ref[...] + gain * residual
        direction_ref[...] = direction
        solution_ref[...] = solution_ref[...] + direction
        high, low = halves(direction)
        pair_ref[:, :columns] = high
        pair_ref[:, columns:] = low
        return damping_next

    damping = step(0, 1.0 / ratio, False, False)
    damping = lax.fori_loop(1, ITERS - 1, lambda k, d: step(k, d, False, True), damping)
    step(ITERS - 1, damping, True, True)

    final = residual_ref[...]
    norms_ref[me] = jnp.sum(final * final, axis=0, keepdims=True)

    @pl.loop(1, devices)
    def _(step):
        other = lax.rem(me + step, devices)
        pltpu.make_async_remote_copy(
            src_ref=norms_ref.at[me], dst_ref=norms_ref.at[me],
            send_sem=norm_send, recv_sem=norm_recv,
            device_id=(other // n_sub, lax.rem(other, n_sub)), device_id_type=MESH,
        ).start()

    for slot in range(1, ITERS):
        for j in range(4):
            exchange(slot, j).wait_send()
    others = norms_ref.at[pl.ds(0, devices - 1)]
    pltpu.make_async_copy(others, others, norm_recv).wait()
    pltpu.make_async_copy(others, others, norm_send).wait()
    norm_ref[...] = jnp.sqrt(jnp.sum(norms_ref[...], axis=0))


def solution(mesh):
    n_patch, n_sub = mesh.shape["patch"], mesh.shape["sub"]

    def on_device(sources, diag_coef, tiles, tile_cols, send_rows, recv_rows, bounds):
        blk_rows, per_row, size, _ = tiles.shape
        rows = diag_coef.shape[0]
        columns = sources.shape[0]
        sent = send_rows.shape[2]
        halo = recv_rows.shape[1]
        every = 4 * sent + rows
        vmem, smem = pltpu.VMEM, pltpu.SMEM
        result, norm = pl.pallas_call(
            functools.partial(kernel, n_patch, n_sub),
            out_shape=(
                jax.ShapeDtypeStruct((rows, columns), F32),
                jax.ShapeDtypeStruct((1, columns), F32),
            ),
            in_specs=[
                pl.BlockSpec(memory_space=vmem),
                pl.BlockSpec(memory_space=vmem),
                pl.BlockSpec(memory_space=pl.ANY),
                pl.BlockSpec(memory_space=smem),
                pl.BlockSpec(memory_space=vmem),
                pl.BlockSpec(memory_space=vmem),
                pl.BlockSpec(memory_space=smem),
            ],
            out_specs=(pl.BlockSpec(memory_space=vmem), pl.BlockSpec(memory_space=vmem)),
            scratch_shapes=[
                vmem(tiles.shape, F32),
                vmem((every, rows), BF16),
                vmem((every, rows), BF16),
                vmem((every, halo), BF16),
                vmem((every, halo), BF16),
                vmem((rows, halo), BF16),
                vmem((rows, halo), BF16),
                vmem((rows, columns), F32),
                vmem((rows, columns), F32),
                vmem((4 * sent, columns), F32),
                vmem((every, columns), F32),
                vmem((rows, 2 * columns), BF16),
                vmem((4 * sent, 2 * columns), BF16),
                vmem((ITERS, 4, sent, columns), F32),
                vmem((ITERS, 4, sent, columns), F32),
                vmem((4, 1, sent), jnp.int32),
                vmem((n_patch * n_sub, 1, columns), F32),
                pltpu.SemaphoreType.DMA((blk_rows,)),
                pltpu.SemaphoreType.DMA((4,)),
                pltpu.SemaphoreType.DMA((4,)),
                pltpu.SemaphoreType.DMA((ITERS, 4)),
                pltpu.SemaphoreType.DMA((ITERS, 4)),
                pltpu.SemaphoreType.DMA,
                pltpu.SemaphoreType.DMA,
            ],
            compiler_params=pltpu.CompilerParams(collective_id=0, has_side_effects=True),
            name="chebyshev",
        )(
            sources.T,
            diag_coef.reshape(blk_rows, size),
            tiles,
            tile_cols,
            send_rows.reshape(4, 1, sent),
            recv_rows,
            bounds,
        )
        return result, norm.reshape(columns)

    return jax.shard_map(
        on_device,
        mesh=mesh,
        in_specs=(
            P(),
            P(("patch", "sub")),
            P(("patch", "sub"), None, None, None),
            P(("patch", "sub"), None),
            P(("patch", "sub"), None, None),
            P(("patch", "sub"), None),
            P(),
        ),
        out_specs=(P(("patch", "sub"), None), P()),
        check_vma=False,
    )
```

time: 231 us -> 55.7 us (0.24)
  local copies, waits for them, and re-layouts: 78.7 us -> 2.8 us
  starting transfers between devices: 53.4 us -> 0 us
  Pallas kernels: 0 us -> 52.1 us
  blocking collectives: 38.8 us -> 0 us
  matrix products: 28 us -> 0 us
  waiting for transfers between devices: 13.6 us -> 0 us
  other arithmetic: 11.9 us -> 0 us
  between operations: 5.44 us -> 0.64 us
    gather x64 -> x0, local copies, waits for them, and re-layouts: 73.6 us -> none  [the longest x48 54.6 us: operate(): extended[tile_cols[:, slot_index]]]
    ppermute x32 -> x0, starting transfers between devices: 53.4 us -> none  [shifted(): return lax.ppermute(value, axis, pairs)]
    pallas_call x0 -> x1, Pallas kernels: none -> 52.1 us  [on_device(): pl.pallas_call(functools.partial(kernel, n_patch, n_sub), out_shape=(jax....]
    psum x1 -> x0, blocking collectives: 38.8 us -> none  [on_device(): squares = lax.psum(jnp.sum(final * final, axis=0), ('patch', 'sub'))]
    dot_general x48 -> x0, matrix products: 28 us -> none  [operate(): jnp.einsum('bij,bjk->bik', tiles[:, slot_index], extended[tile_cols[:, sl...]
    ppermute x32 -> x0, waiting for transfers between devices: 13.6 us -> none  [shifted(): return lax.ppermute(value, axis, pairs)]
    concatenate x16 -> x0, other arithmetic: 5.91 us -> none  [the longest x8 4.08 us: operate(): jnp.concatenate([field, halo_rows], axis=0).reshape(-1, tile_size, columns)]
    slice x9 -> x0, local copies, waits for them, and re-layouts: 3.37 us -> none  [the longest x8 2.06 us: operate(): below_patch = shifted(packed[1], 'patch', 1)]
  transfers between devices with their start and end apart: 32 -> 0, of which waited for: 13 -> 0; matrix products, arithmetic and copies ran while one was open for 0% -> 0% of each run, Pallas kernels for 0% -> 0%
where the time goes in v1:
time: 55.7 us; the launch traced here: 55.5 us
  Pallas kernels  52.1 us (94%)
  local copies, waits for them, and re-layouts  2.8 us (5%)
  between operations  0.64 us (1%)
    pallas_call x1, Pallas kernels, on_device(): pl.pallas_call(functools.partial(kernel, n_patch, n_sub), out_shape=(jax....  52.1 us
    unnamed x2, local copies, waits for them, and re-layouts  2.8 us

profile of v1, /device:TPU:0, one launch (start us, length us, event | category | flops | bytes accessed | tf_op | source)
XLA Modules:
  0.0 55.5 jit_solution(11200086586122862561)
XLA Ops:
  0.6 52.1 %chebyshev.1 = (f32[512,128]{1,0:T(8,128)}, f32[1,128]{1,0:T(1,128)}) custom-call(s32[2,128]{1,0:T(2,128)} %bitcast.6, f32[4,128]{1,0:T(4,128)} %bitcast.4, f32[4,6,128,128]{3,2,1,0:T(8,128)} %tiles_hbm.1, s32[4,6]{1,0:T(4,128)} %cols_ref.1, s32[4,1,128]{2,1,0:T(1,128)} %bitcast.5, s32[1,512]{1,0:T(1,128)} %receives_ref.1, f32[2]{0:T(128)} %bounds_ref.1), custom_call_target="tpu_custom_call" | custom-call | tf_op jit(solution)/shard_map/chebyshev/pallas_call | solution.py:255
  52.7 1.7 %copy.11 = f32[512,128]{1,0:T(8,128)} copy(f32[512,128]{1,0:T(8,128)} %get-tuple-element.8) | data formatting | bytes 524288
  54.4 1.1 %copy.12 = f32[128]{0:T(128)} copy(f32[128]{0:T(128)} %bitcast.7) | data formatting | bytes 1024

commit v2 on v1

--- a/solution.py
+++ b/solution.py
@@ -30,7 +30,7 @@
     solution_ref, norm_ref,
     tiles_ref, near_hi, near_lo, far_hi, far_lo, halo_hi, halo_lo,
     direction_ref, residual_ref, packed_residual, total_ref, pair_ref, heard_pair,
-    packed_ref, heard_ref, heard_rows, norms_ref,
+    packed_ref, heard_ref, heard_rows, norms_ref, counts_ref, pick_ref, place_ref,
     tile_sems, row_send, row_recv, send_sems, recv_sems, norm_send, norm_recv,
 ):
     blk_rows, per_row, size, _ = tiles_hbm.shape
@@ -80,31 +80,23 @@
         return total
 
     right_side = counted(me * rows + lax.broadcasted_iota(jnp.int32, (rows, columns), 0))
-    direction = right_side / centre
-    residual_ref[...] = right_side
-    direction_ref[...] = direction
-    solution_ref[...] = direction
-    high, low = halves(direction)
-    pair_ref[:, :columns] = high
-    pair_ref[:, columns:] = low
+    counts_ref[...] = right_side
 
     def as_column(row, width):
         return jnp.broadcast_to(row, (width, row.shape[1])).T
 
     picks = []
     for j in range(4):
-        column = as_column(sends_ref[j], columns)
-        mine = counted(me * rows + column)
-        packed_residual[pl.ds(j * sent, sent)] = mine
-        packed_ref[0, j] = mine / centre
         wide = as_column(sends_ref[j], rows)
         picks.append(
             jnp.where(wide == lax.broadcasted_iota(jnp.int32, (sent, rows), 1), 1.0, 0.0).astype(BF16)
         )
-    pick = jnp.concatenate(picks, axis=0)
-    place = jnp.where(
-        receives_ref[...] == lax.broadcasted_iota(jnp.int32, (packed_rows, halo), 0), 1.0, 0.0
-    ).astype(BF16)
+    pick_ref[...] = jnp.concatenate(picks, axis=0)
+    for i in range(halo // size):
+        wide = as_column(receives_ref[:, i * size : (i + 1) * size], packed_rows)
+        place_ref[pl.ds(i * size, size)] = jnp.where(
+            wide == lax.broadcasted_iota(jnp.int32, (size, packed_rows), 1), 1.0, 0.0
+        ).astype(BF16)
 
     pl.semaphore_wait(barrier, devices - 1)
     row_copies = []
@@ -139,21 +131,16 @@
                 halo_lo[pl.ds(b * size, size), place_at] = low
     own = pl.ds(packed_rows, rows)
     first = pl.ds(0, packed_rows)
-    for halo_part, far, near in ((halo_hi, far_hi, near_hi), (halo_lo, far_lo, near_lo)):
-        far[own] = lax.dot_general(
-            halo_part[...], place, (((1,), (1,)), ((), ())), preferred_element_type=F32
-        ).astype(BF16)
-        far[first] = jnp.dot(pick, far[own], preferred_element_type=F32).astype(BF16)
-        near[first] = jnp.dot(pick, near[own], preferred_element_type=F32).astype(BF16)
-
+
+    heard_counts = []
     for j in range(4):
         row_copies[j].wait()
     for j in range(4):
         base = (origins[j][0] * n_sub + origins[j][1]) * rows
-        value = counted(base + as_column(heard_rows[j], columns)) / centre
-        high, low = halves(value)
-        heard_pair[pl.ds(j * sent, sent), :columns] = high
-        heard_pair[pl.ds(j * sent, sent), columns:] = low
+        heard_counts.append(counted(base + as_column(heard_rows[j], columns)).astype(BF16))
+    halo_counts = jnp.dot(
+        place_ref[...], jnp.concatenate(heard_counts, axis=0), preferred_element_type=F32
+    ).astype(BF16)
 
     def exchange(slot, j):
         return pltpu.make_async_remote_copy(
@@ -181,20 +168,20 @@
     def far_product(at, part):
         return product(far_hi[at, part], far_lo[at, part], heard_pair[part], columns)
 
-    def step(slot, damping, last, heard):
+    def advance(damping):
+        damping_next = 1.0 / (2.0 * ratio - damping)
+        return damping_next, damping_next * damping, 2.0 * damping_next / half_width
+
+    def step(slot, damping, last):
         at = own if last else pl.ds(0, packed_rows + rows)
         total_ref[at] = product(near_hi[at], near_lo[at], pair_ref[...], columns)
-        if heard:
-            listen(slot, (2, 3))
+        listen(slot, (2, 3))
         total_ref[at] = total_ref[at] + far_product(at, sub_part)
-        if heard:
-            listen(slot, (0, 1))
+        listen(slot, (0, 1))
         if last:
             residual_ref[...] = residual_ref[...] - (total_ref[own] + far_product(own, patch_part))
             return damping
-        damping_next = 1.0 / (2.0 * ratio - damping)
-        keep = damping_next * damping
-        gain = 2.0 * damping_next / half_width
+        damping_next, keep, gain = advance(damping)
         for group in (0, 2):
             span = pl.ds(group * sent, 2 * sent)
             update = total_ref[span] + far_product(span, patch_part)
@@ -216,9 +203,45 @@
         pair_ref[:, columns:] = low
         return damping_next
 
-    damping = step(0, 1.0 / ratio, False, False)
-    damping = lax.fori_loop(1, ITERS - 1, lambda k, d: step(k, d, False, True), damping)
-    step(ITERS - 1, damping, True, True)
+    counts = counts_ref[...].astype(BF16)
+    product_sum = (
+        jnp.dot(near_hi[own], counts, preferred_element_type=F32)
+        + jnp.dot(near_lo[own], counts, preferred_element_type=F32)
+        + jnp.dot(halo_hi[...], halo_counts, preferred_element_type=F32)
+        + jnp.dot(halo_lo[...], halo_counts, preferred_element_type=F32)
+    )
+    right_side = counts_ref[...]
+    residual = right_side - product_sum / centre
+    damping, keep, gain = advance(1.0 / ratio)
+    before = right_side / centre
+    direction = keep * before + gain * residual
+    high, low = halves(direction)
+    pair_ref[:, :columns] = high
+    pair_ref[:, columns:] = low
+    for group in (0, 2):
+        wide = jnp.dot(
+            pick_ref[pl.ds(group * sent, 2 * sent)], pair_ref[...], preferred_element_type=F32
+        )
+        wide = wide[:, :columns] + wide[:, columns:]
+        for i in range(2):
+            packed_ref[1, group + i] = wide[i * sent : (i + 1) * sent]
+            exchange(1, group + i).start()
+    residual_ref[...] = residual
+    direction_ref[...] = direction
+    solution_ref[...] = before + direction
+    high, low = halves(residual)
+    wide = jnp.dot(pick_ref[...], jnp.concatenate([high, low], axis=1), preferred_element_type=F32)
+    packed_residual[...] = wide[:, :columns] + wide[:, columns:]
+
+    for halo_part, far, near in ((halo_hi, far_hi, near_hi), (halo_lo, far_lo, near_lo)):
+        far[own] = jnp.dot(
+            halo_part[...], place_ref[...], preferred_element_type=F32
+        ).astype(BF16)
+        far[first] = jnp.dot(pick_ref[...], far[own], preferred_element_type=F32).astype(BF16)
+        near[first] = jnp.dot(pick_ref[...], near[own], preferred_element_type=F32).astype(BF16)
+
+    damping = lax.fori_loop(1, ITERS - 1, lambda k, d: step(k, d, False), damping)
+    step(ITERS - 1, damping, True)
 
     final = residual_ref[...]
     norms_ref[me] = jnp.sum(final * final, axis=0, keepdims=True)
@@ -238,6 +261,11 @@
     others = norms_ref.at[pl.ds(0, devices - 1)]
     pltpu.make_async_copy(others, others, norm_recv).wait()
     pltpu.make_async_copy(others, others, norm_send).wait()
+    norm_ref[...] = norms_ref[...]
+
+
+def finish(solution_ref, norms_ref, result_ref, norm_ref):
+    result_ref[...] = solution_ref[...]
     norm_ref[...] = jnp.sqrt(jnp.sum(norms_ref[...], axis=0))
 
 
@@ -252,11 +280,11 @@
         halo = recv_rows.shape[1]
         every = 4 * sent + rows
         vmem, smem = pltpu.VMEM, pltpu.SMEM
-        result, norm = pl.pallas_call(
+        held, norms = pl.pallas_call(
             functools.partial(kernel, n_patch, n_sub),
             out_shape=(
                 jax.ShapeDtypeStruct((rows, columns), F32),
-                jax.ShapeDtypeStruct((1, columns), F32),
+                jax.ShapeDtypeStruct((n_patch * n_sub, 1, columns), F32),
             ),
             in_specs=[
                 pl.BlockSpec(memory_space=vmem),
@@ -286,6 +314,9 @@
                 vmem((ITERS, 4, sent, columns), F32),
                 vmem((4, 1, sent), jnp.int32),
                 vmem((n_patch * n_sub, 1, columns), F32),
+                vmem((rows, columns), F32),
+                vmem((4 * sent, rows), BF16),
+                vmem((halo, 4 * sent), BF16),
                 pltpu.SemaphoreType.DMA((blk_rows,)),
                 pltpu.SemaphoreType.DMA((4,)),
                 pltpu.SemaphoreType.DMA((4,)),
@@ -305,6 +336,16 @@
             recv_rows,
             bounds,
         )
+        result, norm = pl.pallas_call(
+            finish,
+            out_shape=(
+                jax.ShapeDtypeStruct((rows, columns), F32),
+                jax.ShapeDtypeStruct((1, columns), F32),
+            ),
+            in_specs=[pl.BlockSpec(memory_space=vmem)] * 2,
+            out_specs=(pl.BlockSpec(memory_space=vmem), pl.BlockSpec(memory_space=vmem)),
+            name="finish",
+        )(held, norms)
         return result, norm.reshape(columns)
 
     return jax.shard_map(

time: 55.7 us -> 55.2 us (level)
  local copies, waits for them, and re-layouts: 2.8 us -> 0 us
  Pallas kernels: 52.1 us -> 54.4 us
    unnamed x2 -> x0, local copies, waits for them, and re-layouts: 2.8 us -> none
    pallas_call x0 -> x1, Pallas kernels: none -> 1.68 us  [on_device(): pl.pallas_call(finish, out_shape=(jax.ShapeDtypeStruct((rows, columns), F...]
    pallas_call x1, Pallas kernels: 52.1 us -> 52.7 us  [on_device(): pl.pallas_call(functools.partial(kernel, n_patch, n_sub), out_shape=(jax....]
where the time goes in v2:
time: 55.2 us; the launch traced here: 55 us
  Pallas kernels  54.4 us (99%)
  between operations  0.64 us (1%)
    pallas_call x1, Pallas kernels, on_device(): pl.pallas_call(functools.partial(kernel, n_patch, n_sub), out_shape=(jax....  52.7 us
    pallas_call x1, Pallas kernels, on_device(): pl.pallas_call(finish, out_shape=(jax.ShapeDtypeStruct((rows, columns), F...  1.68 us

profile of v2, /device:TPU:0, one launch (start us, length us, event | category | flops | bytes accessed | tf_op | source)
XLA Modules:
  0.0 55.0 jit_solution(1133245295481332621)
XLA Ops:
  0.6 52.7 %chebyshev.1 = (f32[512,128]{1,0:T(8,128)}, f32[32,1,128]{2,1,0:T(1,128)}) custom-call(s32[2,128]{1,0:T(2,128)} %bitcast.6, f32[4,128]{1,0:T(4,128)} %bitcast.4, f32[4,6,128,128]{3,2,1,0:T(8,128)} %tiles_hbm.1, s32[4,6]{1,0:T(4,128)} %cols_ref.1, s32[4,1,128]{2,1,0:T(1,128)} %bitcast.5, s32[1,512]{1,0:T(1,128)} %receives_ref.1, f32[2]{0:T(128)} %bounds_ref.1), custom_call_target="tpu_custom_call" | custom-call | tf_op jit(solution)/shard_map/chebyshev/pallas_call | solution.py:283
  53.3 1.7 %finish.1 = (f32[512,128]{1,0:T(8,128)}, f32[1,128]{1,0:T(1,128)}) custom-call(f32[512,128]{1,0:T(8,128)} %get-tuple-element.6.solution_ref, f32[32,1,128]{2,1,0:T(1,128)} %get-tuple-element.7.norms_ref), custom_call_target="tpu_custom_call" | custom-call | tf_op jit(solution)/shard_map/finish/pallas_call | solution.py:339

commit v3 on v2

--- a/solution.py
+++ b/solution.py
@@ -31,6 +31,7 @@
     tiles_ref, near_hi, near_lo, far_hi, far_lo, halo_hi, halo_lo,
     direction_ref, residual_ref, packed_residual, total_ref, pair_ref, heard_pair,
     packed_ref, heard_ref, heard_rows, norms_ref, counts_ref, pick_ref, place_ref,
+    message_ref, echo_out, echo_in, echo_hi, echo_lo, echo_sems,
     tile_sems, row_send, row_recv, send_sems, recv_sems, norm_send, norm_recv,
 ):
     blk_rows, per_row, size, _ = tiles_hbm.shape
@@ -153,7 +154,7 @@
         return pltpu.make_async_remote_copy(
             src_ref=packed_ref.at[slot, j], dst_ref=heard_ref.at[slot, j],
             send_sem=send_sems.at[slot, j], recv_sem=recv_sems.at[slot, j],
-            device_id=targets[j], device_id_type=MESH,
+            device_id=targets[0], device_id_type=MESH,
         )
 
     patch_part, sub_part = pl.ds(0, 2 * sent), pl.ds(2 * sent, 2 * sent)
@@ -172,27 +173,58 @@
         damping_next = 1.0 / (2.0 * ratio - damping)
         return damping_next, damping_next * damping, 2.0 * damping_next / half_width
 
-    def step(slot, damping, last):
+    distant = lax.rem(patch, 2)
+    close = 1 - distant
+    distant_part = pl.ds(pl.multiple_of(distant * sent, sent), sent)
+    close_part = pl.ds(pl.multiple_of(close * sent, sent), sent)
+
+    def patch_copy(source, slot, j):
+        return pltpu.make_async_remote_copy(
+            src_ref=source, dst_ref=heard_ref.at[slot, 1 - j],
+            send_sem=send_sems.at[slot, j], recv_sem=recv_sems.at[slot, 1 - j],
+            device_id=(lax.rem(patch + n_patch + 2 * j - 1, n_patch), sub), device_id_type=MESH,
+        )
+
+    def step(slot, damping, gain_before, last):
         at = own if last else pl.ds(0, packed_rows + rows)
         total_ref[at] = product(near_hi[at], near_lo[at], pair_ref[...], columns)
+        high, low = halves(packed_ref[slot - 1, distant])
+        echo = gain_before * product(
+            echo_hi[...], echo_lo[...], jnp.concatenate([high, low], axis=1), columns
+        )
         listen(slot, (2, 3))
         total_ref[at] = total_ref[at] + far_product(at, sub_part)
-        listen(slot, (0, 1))
+        arrival(slot, close).wait_recv()
+        high, low = halves(heard_ref[slot, close])
+        heard_pair[close_part, :columns] = high
+        heard_pair[close_part, columns:] = low
+        if not last:
+            damping_next, keep, gain = advance(damping)
+            total = total_ref[distant_part] + far_product(distant_part, close_part)
+            message_ref[slot + 1] = keep * packed_ref[slot, distant] + gain * (
+                packed_residual[distant_part] - total
+            )
+            patch_copy(message_ref.at[slot + 1], slot + 1, distant).start()
+        arrival(slot, distant).wait_recv()
+        high, low = halves(heard_ref[slot, distant] - echo)
+        heard_pair[distant_part, :columns] = high
+        heard_pair[distant_part, columns:] = low
         if last:
             residual_ref[...] = residual_ref[...] - (total_ref[own] + far_product(own, patch_part))
-            return damping
-        damping_next, keep, gain = advance(damping)
+            return
         for group in (0, 2):
             span = pl.ds(group * sent, 2 * sent)
-            update = total_ref[span] + far_product(span, patch_part)
-            rest = packed_residual[span] - update
+            rest = packed_residual[span] - (total_ref[span] + far_product(span, patch_part))
             packed_residual[span] = rest
             for i in range(2):
-                j = group + i
-                packed_ref[slot + 1, j] = (
-                    keep * packed_ref[slot, j] + gain * rest[i * sent : (i + 1) * sent]
+                packed_ref[slot + 1, group + i] = (
+                    keep * packed_ref[slot, group + i] + gain * rest[i * sent : (i + 1) * sent]
                 )
-                exchange(slot + 1, j).start()
+            if group == 0:
+                patch_copy(packed_ref.at[slot + 1, close], slot + 1, close).start()
+            else:
+                exchange(slot + 1, 2).start()
+                exchange(slot + 1, 3).start()
         residual = residual_ref[...] - (total_ref[own] + far_product(own, patch_part))
         residual_ref[...] = residual
         direction = keep * direction_ref[...] + gain * residual
@@ -201,7 +233,7 @@
         high, low = halves(direction)
         pair_ref[:, :columns] = high
         pair_ref[:, columns:] = low
-        return damping_next
+        return damping_next, gain
 
     counts = counts_ref[...].astype(BF16)
     product_sum = (
@@ -240,8 +272,23 @@
         far[first] = jnp.dot(pick_ref[...], far[own], preferred_element_type=F32).astype(BF16)
         near[first] = jnp.dot(pick_ref[...], near[own], preferred_element_type=F32).astype(BF16)
 
-    damping = lax.fori_loop(1, ITERS - 1, lambda k, d: step(k, d, False), damping)
-    step(ITERS - 1, damping, True)
+    echo_out[...] = far_hi[distant_part, distant_part].astype(F32) + far_lo[
+        distant_part, distant_part
+    ].astype(F32)
+    echo_copy = pltpu.make_async_remote_copy(
+        src_ref=echo_out, dst_ref=echo_in, send_sem=echo_sems.at[0], recv_sem=echo_sems.at[1],
+        device_id=(lax.rem(patch + n_patch + 2 * distant - 1, n_patch), sub), device_id_type=MESH,
+    )
+    echo_copy.start()
+    for j in range(2):
+        packed_ref[0, j] = jnp.zeros((sent, columns), F32)
+    echo_hi[...] = jnp.zeros((sent, sent), BF16)
+    echo_lo[...] = jnp.zeros((sent, sent), BF16)
+    state = step(1, damping, jnp.zeros((1, columns), F32), False)
+    echo_copy.wait()
+    echo_hi[...], echo_lo[...] = halves(echo_in[...])
+    damping, gain = lax.fori_loop(2, ITERS - 1, lambda k, state: step(k, *state, False), state)
+    step(ITERS - 1, damping, gain, True)
 
     final = residual_ref[...]
     norms_ref[me] = jnp.sum(final * final, axis=0, keepdims=True)
@@ -317,6 +364,12 @@
                 vmem((rows, columns), F32),
                 vmem((4 * sent, rows), BF16),
                 vmem((halo, 4 * sent), BF16),
+                vmem((ITERS, sent, columns), F32),
+                vmem((sent, sent), F32),
+                vmem((sent, sent), F32),
+                vmem((sent, sent), BF16),
+                vmem((sent, sent), BF16),
+                pltpu.SemaphoreType.DMA((2,)),
                 pltpu.SemaphoreType.DMA((blk_rows,)),
                 pltpu.SemaphoreType.DMA((4,)),
                 pltpu.SemaphoreType.DMA((4,)),

time: 55.2 us -> 54.4 us (0.986)
  Pallas kernels: 54.4 us -> 53.5 us
    pallas_call x1, Pallas kernels: 52.7 us -> 51.9 us  [on_device(): pl.pallas_call(functools.partial(kernel, n_patch, n_sub), out_shape=(jax....]
where the time goes in v3:
time: 54.4 us; the launch traced here: 54.2 us
  Pallas kernels  53.5 us (98%)
  between operations  0.64 us (1%)
    pallas_call x1, Pallas kernels, on_device(): pl.pallas_call(functools.partial(kernel, n_patch, n_sub), out_shape=(jax....  51.9 us
    pallas_call x1, Pallas kernels, on_device(): pl.pallas_call(finish, out_shape=(jax.ShapeDtypeStruct((rows, columns), F...  1.68 us

profile of v3, /device:TPU:0, one launch (start us, length us, event | category | flops | bytes accessed | tf_op | source)
XLA Modules:
  0.0 54.2 jit_solution(15956998085446926968)
XLA Ops:
  0.6 51.9 %chebyshev.1 = (f32[512,128]{1,0:T(8,128)}, f32[32,1,128]{2,1,0:T(1,128)}) custom-call(s32[2,128]{1,0:T(2,128)} %bitcast.6, f32[4,128]{1,0:T(4,128)} %bitcast.4, f32[4,6,128,128]{3,2,1,0:T(8,128)} %tiles_hbm.1, s32[4,6]{1,0:T(4,128)} %cols_ref.1, s32[4,1,128]{2,1,0:T(1,128)} %bitcast.5, s32[1,512]{1,0:T(1,128)} %receives_ref.1, f32[2]{0:T(128)} %bounds_ref.1), custom_call_target="tpu_custom_call" | custom-call | tf_op jit(solution)/shard_map/chebyshev/pallas_call | solution.py:330
  52.5 1.7 %finish.1 = (f32[512,128]{1,0:T(8,128)}, f32[1,128]{1,0:T(1,128)}) custom-call(f32[512,128]{1,0:T(8,128)} %get-tuple-element.6.solution_ref, f32[32,1,128]{2,1,0:T(1,128)} %get-tuple-element.7.norms_ref), custom_call_target="tpu_custom_call" | custom-call | tf_op jit(solution)/shard_map/finish/pallas_call | solution.py:392
